TPU v7x, 32 devices: a whole 2x2x4 slice. The times are simulated.
32 devices in a mesh: rep: 2 (over x), exp: 2 (over core), tp: 8 (over z, y).
Axes of the slice: x: 2, y: 2, z: 4, core: 2. Of those that a mesh axis runs over, the one named last changes fastest.
Arguments:
- tokens: bfloat16 [1024, 4096], P(('rep', 'exp'), 'tp'), parts along dimension 0
- smooth_in: float32 [4096], P('tp'), may hold values from 0.5 to 2
- expert_ids: int32 [1024, 2], P(('rep', 'exp')), parts along dimension 0, may hold values from 0 to 3, as said below
- gate_fixed: int32 [1024, 2], P(('rep', 'exp')), parts along dimension 0, may hold values from 1 to 32767
- slots: int32 [1024, 2], P(('rep', 'exp')), parts along dimension 0, may hold values from 0 to 255, as said below
- w_gate: bfloat16 [4, 4096, 7168], P('exp', None, 'tp')
- w_up: bfloat16 [4, 4096, 7168], P('exp', None, 'tp')
- w_down: bfloat16 [4, 7168, 4096], P('exp', 'tp')
- gate_scale: float32 [4, 7168], P('exp', 'tp'), may hold values from 0.00010557433 to 0.0004222973
- up_scale: float32 [4, 7168], P('exp', 'tp'), may hold values from 0.00010557433 to 0.0004222973
- smooth_mid: float32 [4, 7168], P('exp', 'tp'), may hold values from 0.5 to 2
- down_scale: float32 [4, 4096], P('exp'), may hold values from 0.00015961338 to 0.0006384535
Outputs:
- moe_out: bfloat16 [1024, 4096], P(('rep', 'exp'), 'tp'), parts along dimension 0
There are 2 independent parts, one for each index of `rep`. A program takes and returns all parts, laid end to end along the dimension named above; an argument that names none is the same for every part. Nothing has to cross between parts.
Inputs may be any that keep to these rules, and one draw needn't show every extreme that they name: `expert_ids`: the two experts of a token differ. Within one aligned block of 256 tokens (the tokens of one index of exp), the slots of the pairs that name one expert are distinct and run from 0 to their number less one. In every block some expert is named by 192 or more tokens.
All inputs are finite; a program needn't handle non-finite values.
Results may differ from a plain program's by a relative error of at most 0.006.
Values may be sent and summed in bfloat16 or wider, within the bound.
A program may use at most 128 MiB of HBM per device.

v0:
```python
import functools

import jax
import jax.numpy as jnp
from jax import lax
from jax.experimental import pallas as pl
from jax.experimental.pallas import tpu as pltpu
from jax.sharding import PartitionSpec as P

CLIP_RATIO = 0.35
EPSILON = 1e-06
LANES = 128
MESH = pl.DeviceIdType.MESH
F32 = jnp.float32
BF16 = jnp.bfloat16


def kernel(
    n, slots,
    tok_ref, smooth_ref, share_ref, wg_ref, wu_ref, wd_ref, gs_ref, us_ref, sm_ref, ds_ref,
    out_ref,
    x, wbuf, dbuf, acc, hq, meta, coef, pk, hx, hm, own, ssend, srecv, ysend, yrecv, comb, zsend, zrecv,
    w_sem, d_sem, pk_s, pk_r, hx_s, hx_r, meta_s, meta_r,
    az_s, ay_s, as_s, ag_r, as_r, rs_s, rs_r, ry_s, ry_r, rz_s, rz_r,
):
    q = n // 2
    me = lax.axis_index("tp")
    core = lax.axis_index("exp")
    z, y = me // 2, me % 2
    direction = 1 - 2 * (z % 2)
    experts = wg_ref.shape[0]
    block, depth = tok_ref.shape
    width = wg_ref.shape[2]

    def z_of(j):
        return (z + direction * j + q) % q

    def chunk(j, other):
        row = y + other * (1 - 2 * y)
        return z_of(j) * 2 + row

    def remote(src, dst, send, recv, device):
        return pltpu.make_async_remote_copy(
            src_ref=src, dst_ref=dst, send_sem=send, recv_sem=recv,
            device_id=device, device_id_type=MESH,
        )

    sibling = {"exp": 1 - core}
    partner = {"tp": chunk(0, 1)}

    def weight_copies(k):
        rows = pl.ds(pl.multiple_of(chunk(k // 2, k % 2) * depth, depth), depth)
        slot = k % slots
        return [
            pltpu.make_async_copy(ref.at[:, rows, :], wbuf.at[slot, i], w_sem.at[slot, i])
            for i, ref in enumerate((wg_ref, wu_ref))
        ]

    def down_copy(p):
        cols = pl.ds(pl.multiple_of(p * depth, depth), depth)
        return pltpu.make_async_copy(wd_ref.at[:, :, cols], dbuf.at[p], d_sem.at[p])

    for k in range(slots):
        for copy in weight_copies(k):
            copy.start()

    barrier = pltpu.get_barrier_semaphore()
    pl.semaphore_signal(barrier, inc=1, device_id=sibling, device_id_type=MESH)

    @pl.loop(1, n)
    def _(d):
        pl.semaphore_signal(barrier, inc=1, device_id={"tp": (me + d) % n}, device_id_type=MESH)

    smoothed = tok_ref[...].astype(F32) / smooth_ref[...]
    peak = jnp.max(jnp.abs(smoothed), axis=1, keepdims=True)
    peak_row = jnp.broadcast_to(peak, (block, LANES)).T[0:1, :]
    pk[pl.ds(me, 1)] = peak_row[None]

    pl.semaphore_wait(barrier, n)

    def pk_copy(d):
        return remote(pk.at[me], pk.at[me], pk_s.at[d], pk_r.at[me], {"tp": (me + d) % n})

    @pl.loop(1, n)
    def _(d):
        pk_copy(d).start()

    @pl.loop(0, 2 * experts)
    def _(t):
        acc[t] = jnp.zeros(acc.shape[1:], F32)

    @pl.loop(1, n)
    def _(d):
        p = (me + d) % n
        remote(pk.at[p], pk.at[p], pk_s.at[d], pk_r.at[p], {"tp": p}).wait_recv()

    row_peak = jnp.max(pk[0:n], axis=0)
    peak_col = jnp.broadcast_to(row_peak, (LANES, block)).T
    in_scale = CLIP_RATIO * (peak_col + EPSILON) / 127.0
    smoothed = tok_ref[...].astype(F32) / smooth_ref[...]
    x[me, core] = jnp.clip(smoothed / in_scale[:, 0:1], -127.0, 127.0).astype(BF16)
    lane = lax.broadcasted_iota(jnp.int32, (block, LANES), 1)
    meta[core] = jnp.where(lane < 2 * experts, share_ref[...], in_scale)

    def z_copy(j):
        return remote(x.at[me, core], x.at[me, core], az_s.at[j], ag_r.at[me], {"tp": chunk(j, 0)})

    def y_copy(j):
        p = chunk(j, 0)
        return remote(x.at[p, core], x.at[p, core], ay_s.at[j], ag_r.at[p], partner)

    def sib_copy(p, b):
        return remote(x.at[p, b], x.at[p, b], as_s.at[p], as_r.at[p], sibling)

    def arrived(p):
        remote(x.at[p, core], x.at[p, core], as_s.at[p], ag_r.at[p], sibling).wait_recv()

    y_copy(0).start()

    @pl.loop(1, q)
    def _(j):
        z_copy(j).start()

    meta_copy = remote(meta.at[core], meta.at[core], meta_s, meta_r, sibling)
    meta_copy.start()
    sib_copy(me, core).start()

    def compute(k):
        p = chunk(k // 2, k % 2)
        slot = k % slots
        for copy in weight_copies(k):
            copy.wait()
        sib_copy(p, 1 - core).wait_recv()

        @pl.loop(0, 2 * experts)
        def _(t):
            acc[t] += jnp.dot(
                x[p].reshape(2 * block, depth), wbuf[slot, t // experts, t % experts],
                preferred_element_type=F32,
            )

        @pl.when(k + slots < n)
        def _():
            for copy in weight_copies(k + slots):
                copy.start()

        down_copy(p).start()

    compute(0)
    arrived(chunk(0, 1))
    sib_copy(chunk(0, 1), core).start()

    @pl.loop(1, q)
    def _(j):
        p = chunk(j, 0)
        arrived(p)
        y_copy(j).start()
        sib_copy(p, core).start()
        compute(2 * j - 1)
        compute(2 * j)
        p = chunk(j, 1)
        arrived(p)
        sib_copy(p, core).start()

    compute(n - 1)
    meta_copy.wait_recv()

    rb = 32
    blocks = block // rb
    for e in range(experts):

        @pl.loop(0, 2 * blocks)
        def _(r):
            rows = pl.ds(pl.multiple_of(r * rb, rb), rb)
            inner = pl.ds(pl.multiple_of((r % blocks) * rb, rb), rb)
            scale = meta[r // blocks, inner, :][:, LANES - 1:]
            gate = acc[e, rows, :] * scale * gs_ref[...][e:e + 1]
            up = acc[experts + e, rows, :] * scale * us_ref[...][e:e + 1]
            hidden = gate / (1.0 + jnp.exp(-gate)) * up / sm_ref[...][e:e + 1]
            acc[e, rows, :] = hidden
            hm[rows, :] = jnp.broadcast_to(jnp.max(jnp.abs(hidden), axis=1, keepdims=True), (rb, LANES))

        hx[pl.ds(me, 1), e:e + 1, :] = hm[...].T[0:1, :][None]

    def hx_copy(d):
        return remote(hx.at[me], hx.at[me], hx_s.at[d], hx_r.at[me], {"tp": (me + d) % n})

    @pl.loop(1, n)
    def _(d):
        hx_copy(d).start()

    @pl.loop(1, n)
    def _(d):
        p = (me + d) % n
        remote(hx.at[p], hx.at[p], hx_s.at[d], hx_r.at[p], {"tp": p}).wait_recv()

    mid_rows = CLIP_RATIO * (jnp.max(hx[0:n], axis=0) + EPSILON) / 127.0
    for e in range(experts):
        coef[e] = jnp.broadcast_to(mid_rows[e:e + 1, :], (LANES, 2 * block)).T

        @pl.loop(0, 2 * blocks)
        def _(r):
            rows = pl.ds(pl.multiple_of(r * rb, rb), rb)
            inner = pl.ds(pl.multiple_of((r % blocks) * rb, rb), rb)
            mid = coef[e, rows, :]
            hq[e, rows, :] = jnp.clip(acc[e, rows, :] * (1.0 / mid[:, 0:1]), -127.0, 127.0).astype(BF16)
            lanes = lax.broadcasted_iota(jnp.int32, (rb, LANES), 1)
            picked = jnp.where(lanes == core * experts + e, meta[r // blocks, inner, :], 0.0)
            coef[e, rows, :] = mid * jnp.sum(picked, axis=1, keepdims=True)

    def partial(p, b):
        rows = pl.ds(pl.multiple_of(b * block, block), block)
        cols = pl.ds(pl.multiple_of(p * depth, depth), depth)
        total = None
        for e in range(experts):
            part = jnp.dot(hq[e, rows, :], dbuf[p, e], preferred_element_type=F32)
            part = part * coef[e, rows, 0:1] * ds_ref[:, cols][e:e + 1]
            total = part if total is None else total + part
        return total

    def shard_of(k):
        return chunk(q - 1 - k % q, 1 - k // q)

    def rs_copy(k):
        return remote(ssend.at[k], srecv.at[k], rs_s.at[k], rs_r.at[k], sibling)

    def ry_copy(j):
        return remote(ysend.at[j], yrecv.at[j], ry_s.at[j], ry_r.at[j], partner)

    def rz_copy(j):
        return remote(zsend.at[j], zrecv.at[z], rz_s.at[j], rz_r.at[z], {"tp": chunk(j, 0)})

    def combine(k):
        j = q - 1 - k % q
        rs_copy(k).wait_recv()

        @pl.when(k < q)
        def _():
            ysend[j] = (own[k % 2] + srecv[k].astype(F32)).astype(BF16)
            ry_copy(j).start()

        @pl.when(k >= q)
        def _():
            comb[j] = own[k % 2] + srecv[k].astype(F32)

    @pl.loop(0, n)
    def _(k):
        p = shard_of(k)
        down_copy(p).wait()
        ssend[k] = partial(p, 1 - core).astype(BF16)
        rs_copy(k).start()
        own[k % 2] = partial(p, core)

        @pl.when(k > 0)
        def _():
            combine(k - 1)

    combine(n - 1)

    @pl.loop(0, q - 1)
    def _(i):
        j = q - 1 - i
        ry_copy(j).wait_recv()
        zsend[j] = (comb[j] + yrecv[j].astype(F32)).astype(BF16)
        rz_copy(j).start()

    ry_copy(0).wait_recv()
    comb[0] += yrecv[0].astype(F32)

    @pl.loop(1, q)
    def _(j):
        s = z_of(j)
        remote(zsend.at[j], zrecv.at[s], rz_s.at[j], rz_r.at[s], sibling).wait_recv()
        comb[0] += zrecv[s].astype(F32)

    out_ref[...] = comb[0].astype(BF16)

    meta_copy.wait_send()

    @pl.loop(1, n)
    def _(d):
        pk_copy(d).wait_send()
        hx_copy(d).wait_send()

    @pl.loop(0, n)
    def _(k):
        sib_copy(k, core).wait_send()
        rs_copy(k).wait_send()

    @pl.loop(0, q)
    def _(j):
        y_copy(j).wait_send()
        ry_copy(j).wait_send()

    @pl.loop(1, q)
    def _(j):
        z_copy(j).wait_send()
        rz_copy(j).wait_send()


def per_device(
    n,
    tokens, smooth_in, expert_ids, gate_fixed, slots,
    w_gate, w_up, w_down, gate_scale, up_scale, smooth_mid, down_scale,
):
    q = n // 2
    experts, _, width = w_gate.shape
    block, depth = tokens.shape
    capacity = 3 * block // 4
    gate_values = gate_fixed.astype(F32)
    weight = gate_values / jnp.sum(gate_values, axis=1, keepdims=True)
    pair_weight = jnp.where(slots < capacity, weight, 0.0)
    lane = jnp.arange(LANES, dtype=jnp.int32)[None, :]
    share = sum(
        jnp.where(expert_ids[:, k:k + 1] == lane, pair_weight[:, k:k + 1], 0.0)
        for k in range(expert_ids.shape[1])
    )
    ring = min(n, 5)
    vmem = pl.BlockSpec(memory_space=pltpu.VMEM)
    hbm = pl.BlockSpec(memory_space=pl.ANY)
    dma = pltpu.SemaphoreType.DMA
    slab = (block, depth)
    return pl.pallas_call(
        functools.partial(kernel, n, ring),
        out_shape=jax.ShapeDtypeStruct(slab, BF16),
        in_specs=[vmem] * 3 + [hbm] * 3 + [vmem] * 4,
        out_specs=vmem,
        scratch_shapes=[
            pltpu.VMEM((n, 2, *slab), BF16),
            pltpu.VMEM((ring, 2, experts, depth, width), BF16),
            pltpu.VMEM((n, experts, width, depth), BF16),
            pltpu.VMEM((2 * experts, 2 * block, width), F32),
            pltpu.VMEM((experts, 2 * block, width), BF16),
            pltpu.VMEM((2, block, LANES), F32),
            pltpu.VMEM((experts, 2 * block, LANES), F32),
            pltpu.VMEM((n + 8, 1, block), F32),
            pltpu.VMEM((n + 8, experts, 2 * block), F32),
            pltpu.VMEM((2 * block, LANES), F32),
            pltpu.VMEM((2, *slab), F32),
            pltpu.VMEM((n, *slab), BF16),
            pltpu.VMEM((n, *slab), BF16),
            pltpu.VMEM((q, *slab), BF16),
            pltpu.VMEM((q, *slab), BF16),
            pltpu.VMEM((q, *slab), F32),
            pltpu.VMEM((q, *slab), BF16),
            pltpu.VMEM((q, *slab), BF16),
            dma((ring, 2)), dma((n,)), dma((n,)), dma((n,)), dma((n,)), dma((n,)), dma, dma,
            dma((q,)), dma((q,)), dma((n,)), dma((n,)), dma((n,)),
            dma((n,)), dma((n,)), dma((q,)), dma((q,)), dma((q,)), dma((q,)),
        ],
        compiler_params=pltpu.CompilerParams(
            collective_id=0, has_side_effects=True, vmem_limit_bytes=67043328
        ),
    )(tokens, smooth_in[None, :], share, w_gate, w_up, w_down, gate_scale, up_scale, smooth_mid, down_scale)


def solution(mesh):
    n = mesh.shape["tp"]
    in_specs = (
        P(("rep", "exp"), "tp"),
        P("tp"),
        P(("rep", "exp"), None),
        P(("rep", "exp"), None),
        P(("rep", "exp"), None),
        P("exp", None, "tp"),
        P("exp", None, "tp"),
        P("exp", "tp", None),
        P("exp", "tp"),
        P("exp", "tp"),
        P("exp", "tp"),
        P("exp", None),
    )
    out_specs = P(("rep", "exp"), "tp")
    return jax.shard_map(
        functools.partial(per_device, n), mesh=mesh, in_specs=in_specs, out_specs=out_specs, check_vma=False
    )
```

profile of v0, /device:TPU:0, one launch (start us, length us, event | category | flops | bytes accessed | tf_op | source)
XLA Modules:
  0.0 106.3 jit_solution(6233028246580393184)
XLA Ops:
  0.0 0.7 convert_reduce_fusion
  0.7 0.7 compare_select_fusion
  1.4 0.8 fusion
  2.2 0.9 select_add_fusion.share_ref
  3.0 101.6 %shard_map.118 = bf16[256,512]{1,0:T(8,128)(2,1)} custom-call(bf16[256,512]{1,0:T(8,128)(2,1)} %tok_ref.1, f32[1,512]{1,0:T(1,128)} %bitcast.9, f32[256,128]{1,0:T(8,128)} %select_add_fusion.share_ref, bf16[2,4096,896]{2,1,0:T(8,128)(2,1)} %wg_ref.1, bf16[2,4096,896]{2,1,0:T(8,128)(2,1)} %wu_ref.1, bf16[2,896,4096]{2,1,0:T(8,128)(2,1)} %wd_ref.1, ...), custom_call_target="tpu_custom_call" | custom-call | tf_op jit(solution)/shard_map/pallas_call | solution.py:323
  104.6 1.7 %copy.14 = bf16[256,512]{1,0:T(8,128)(2,1)} copy(bf16[256,512]{1,0:T(8,128)(2,1)} %shard_map.118) | data formatting | bytes 524288
  (1 shorter events, 0.0 us)
where the time goes:
time: 107 us; the launch traced here: 106 us
  Pallas kernels  102 us (95%)
  local copies, waits for them, and re-layouts  2.44 us (2%)
  other arithmetic  2.26 us (2%)
    pallas_call x1, Pallas kernels, per_device(): pl.pallas_call(functools.partial(kernel, n, ring), out_shape=jax.ShapeDty...  102 us

commit v1 on v0

v1 whole, which is shorter than its diff:
```python
import functools

import jax
import jax.numpy as jnp
from jax import lax
from jax.experimental import pallas as pl
from jax.experimental.pallas import tpu as pltpu
from jax.sharding import PartitionSpec as P

CLIP_RATIO = 0.35
EPSILON = 1e-06
LANES = 128
SPLIT = (1, 1)
MESH = pl.DeviceIdType.MESH
F32 = jnp.float32
BF16 = jnp.bfloat16


def kernel(
    n, capacity, sizes,
    tok_ref, smooth_ref, ids_ref, gate_ref, slot_ref, wg_ref, wu_ref, wd_ref, gs_ref, us_ref, sm_ref, ds_ref,
    out_ref,
    x, xq, wbuf, dbuf, acc, h, hq, meta_rows, meta, coef, pk, hx, hm, own, ssend, srecv, comb, yrecv, zrecv,
    w_sem, d_sem, pk_s, pk_r, hx_s, hx_r, meta_s, meta_r,
    ao_s, az_s, ay_s, as_s, ag_r, as_r, rs_s, rs_r, ry_s, ry_r, rz_s, rz_r,
):
    q = n // 2
    me = lax.axis_index("tp")
    core = lax.axis_index("exp")
    z, y = me // 2, me % 2
    direction = 1 - 2 * (z % 2)
    experts, _, width = wg_ref.shape
    block, depth = tok_ref.shape
    groups = len(sizes)
    offsets = [sum(sizes[:g]) for g in range(groups)]
    halves = wbuf.shape[0]
    tiles = [(c, min(LANES, width - c)) for c in range(0, width, LANES)]

    def rows_of(g):
        return pl.ds(offsets[g], sizes[g])

    def z_of(j):
        return (z + direction * j + q) % q

    def chunk(j, other):
        return z_of(j) * 2 + y + other * (1 - 2 * y)

    upper = (2 * z) // q
    near_count = z * (1 - upper) + (q - 1 - z) * upper

    def side(t):
        near = (2 * near_count - t + 4 * q) // (4 * q)
        return near * (1 - 2 * (t % 2)) + (1 - near) * (1 - 2 * upper)

    def line(t):
        near = (2 * near_count - t + 4 * q) // (4 * q)
        return z + side(t) * (near * ((t + 1) // 2) + (1 - near) * (t - near_count))

    def slab(t, other):
        return line(t) * 2 + y + other * (1 - 2 * y)

    def remote(src, dst, send, recv, device):
        return pltpu.make_async_remote_copy(
            src_ref=src, dst_ref=dst, send_sem=send, recv_sem=recv,
            device_id=device, device_id_type=MESH,
        )

    sibling = {"exp": 1 - core}
    partner = {"tp": chunk(0, 1)}

    def chunk_rows(p):
        return pl.ds(pl.multiple_of(p * depth, depth), depth)

    def weight_copies(k):
        rows = chunk_rows(slab(k // 2, k % 2))
        if halves == 1:
            dsts = [wbuf.at[0, :, rows, pl.ds(i * width, width)] for i in range(2)]
        else:
            dsts = [wbuf.at[i, :, rows, :] for i in range(2)]
        return [
            pltpu.make_async_copy(ref.at[:, rows, :], dst, w_sem.at[k, i])
            for i, (ref, dst) in enumerate(zip((wg_ref, wu_ref), dsts))
        ]

    def down_copy(e):
        return pltpu.make_async_copy(wd_ref.at[e], dbuf.at[e], d_sem.at[e])

    barrier = pltpu.get_barrier_semaphore()
    pl.semaphore_signal(barrier, inc=1, device_id=sibling, device_id_type=MESH)

    @pl.loop(1, n)
    def _(d):
        pl.semaphore_signal(barrier, inc=1, device_id={"tp": (me + d) % n}, device_id_type=MESH)

    @pl.loop(0, n)
    def _(k):
        for copy in weight_copies(k):
            copy.start()

    for e in range(experts):
        down_copy(e).start()

    x[me, 0] = tok_ref[...]
    smooth = smooth_ref[...]
    peak = jnp.max(jnp.abs(tok_ref[...].astype(F32) / smooth), axis=1, keepdims=True)
    peak_row = jnp.broadcast_to(peak, (block, LANES)).T[0:1, :]
    pk[pl.ds(me, 1), :, 0:block] = peak_row[None]
    pk[pl.ds(me, 1), :, block:] = smooth[None]

    pl.semaphore_wait(barrier, n)

    def pk_copy(d):
        return remote(pk.at[me], pk.at[me], pk_s.at[d], pk_r.at[me], {"tp": (me + d) % n})

    def piece(g, p, b):
        return x.at[p, b, rows_of(g), :]

    def own_copy(g, up):
        part = piece(g, me, 0)
        return remote(part, part, ao_s.at[g, up], ag_r.at[g, me], {"tp": me + 4 * up - 2})

    def relay_copy(g, p, step):
        part = piece(g, p, 0)
        return remote(part, part, az_s.at[g, p // 2], ag_r.at[g, p], {"tp": me - 2 * step})

    def y_copy(g, p):
        part = piece(g, p, 0)
        return remote(part, part, ay_s.at[g, p // 2], ag_r.at[g, p], partner)

    def sib_copy(g, p):
        return remote(piece(g, p, 0), piece(g, p, 1), as_s.at[g, p], as_r.at[g, p], sibling)

    def arrived(g, p):
        remote(piece(g, p, 0), piece(g, p, 0), as_s.at[g, p], ag_r.at[g, p], sibling).wait_recv()

    def guard_own(act):
        for up, there in enumerate((z > 0, z < q - 1)):

            @pl.when(there)
            def _():
                act(up)

    def guard_slabs(s, act):
        for step in (-1, 1):
            source = z + step * s

            @pl.when((source >= 0) & (source < q))
            def _():
                act(me + 2 * step * s, step)

    def guard_relay(g, p, step, act):
        target = z - step

        @pl.when((target >= 0) & (target < q))
        def _():
            act(relay_copy(g, p, step))

    def begin(g):
        y_copy(g, me).start()
        guard_own(lambda up: own_copy(g, up).start())
        sib_copy(g, me).start()

    def across(g, s):
        def act(p, step):
            arrived(g, p)
            guard_relay(g, p, step, lambda copy: copy.start())
            y_copy(g, p).start()
            sib_copy(g, p).start()

        guard_slabs(s, act)

    def beside(g, t):
        p = slab(t, 1)
        arrived(g, p)
        sib_copy(g, p).start()

    begin(0)

    @pl.loop(1, n)
    def _(d):
        pk_copy(d).start()

    if groups > 1:
        begin(1)

    gates = gate_ref[...].astype(F32)
    total = jnp.sum(gates, axis=0, keepdims=True)
    weight = jnp.where(slot_ref[...] < capacity, gates / total, 0.0)

    def share_of(expert):
        return jnp.sum(jnp.where(ids_ref[...] == expert, weight, 0.0), axis=0, keepdims=True)

    @pl.loop(1, n)
    def _(d):
        p = (me + d) % n
        remote(pk.at[p], pk.at[p], pk_s.at[d], pk_r.at[p], {"tp": p}).wait_recv()

    row_peak = jnp.max(pk[0:n, :, 0:block], axis=0)
    in_scale = CLIP_RATIO * (row_peak + EPSILON) / 127.0
    inverse = 1.0 / in_scale
    for i, owner in enumerate((core, 1 - core)):
        for e in range(experts):
            meta_rows[i, e:e + 1, :] = share_of(owner * experts + e)
        meta_rows[i, experts:experts + 1, :] = in_scale
        meta_rows[i, experts + 1:experts + 2, :] = inverse
    meta_copy = remote(meta_rows.at[1], meta_rows.at[2], meta_s, meta_r, sibling)
    meta_copy.start()
    line_index = lax.broadcasted_iota(jnp.int32, (LANES, block), 0)

    def columns(slot):
        result = jnp.zeros((LANES, block), F32)
        for i in range(experts + 2):
            result = jnp.where(line_index == i, meta_rows[slot, i:i + 1, :], result)
        return result.T

    meta[0] = columns(0)
    meta_copy.wait_recv()
    meta[1] = columns(2)

    def compute(g, k, first):
        p = slab(k // 2, k % 2)
        rg = sizes[g]
        if g == 0:
            for copy in weight_copies(k):
                copy.wait()
        sib_copy(g, p).wait_recv()
        factor = 1.0 / pk[p][:, block:]
        for b in range(2):
            scale = meta[b, rows_of(g), experts + 1:experts + 2]
            scaled = x[p, b, rows_of(g), :].astype(F32) * factor * scale
            xq[b * rg:(b + 1) * rg, :] = jnp.clip(scaled, -127.0, 127.0).astype(BF16)
        for e in range(experts):
            for half in range(halves):
                product = jnp.dot(
                    xq[0:2 * rg, :], wbuf[half, e, chunk_rows(p), :], preferred_element_type=F32
                )
                if first:
                    acc[half, e, 0:2 * rg] = product
                else:
                    acc[half, e, 0:2 * rg] += product

    rb = 32

    def row_blocks(g, body):
        blocks = sizes[g] // rb

        @pl.loop(0, 2 * blocks)
        def _(r):
            rows = pl.ds(pl.multiple_of(r * rb, rb), rb)
            inner = pl.ds(pl.multiple_of(offsets[g] + (r % blocks) * rb, rb), rb)
            body(rows, meta[r // blocks, inner, :])

    def spread(column):
        return jnp.broadcast_to(column, (rb, LANES))

    def hidden(g):
        for e in range(experts):

            def body(rows, info):
                scale = spread(info[:, experts:experts + 1])
                largest = None
                for c, w in tiles:
                    cols = pl.ds(c, w)
                    gate_acc = acc[0, e, rows, cols]
                    up_acc = acc[0, e, rows, pl.ds(width + c, w)] if halves == 1 else acc[1, e, rows, cols]
                    gate = gate_acc * scale[:, 0:w] * gs_ref[:, cols][e:e + 1]
                    factor = us_ref[:, cols][e:e + 1] / sm_ref[:, cols][e:e + 1]
                    up = up_acc * scale[:, 0:w] * factor
                    value = gate / (1.0 + jnp.exp(-gate)) * up
                    h[e, rows, cols] = value
                    size = jnp.abs(value)
                    if w < LANES:
                        size = spread(jnp.max(size, axis=1, keepdims=True))
                    largest = size if largest is None else jnp.maximum(largest, size)
                hm[rows, :] = largest

            row_blocks(g, body)
            hx[g, pl.ds(me, 1), e:e + 1, 0:2 * sizes[g]] = jnp.max(
                hm[0:2 * sizes[g], :].T, axis=0, keepdims=True
            )[None]

        @pl.loop(1, n)
        def _(d):
            hx_copy(g, d).start()

    def hx_copy(g, d):
        return remote(
            hx.at[g, me], hx.at[g, me], hx_s.at[g, d], hx_r.at[g, me], {"tp": (me + d) % n}
        )

    def requantize(g):
        @pl.loop(1, n)
        def _(d):
            p = (me + d) % n
            remote(hx.at[g, p], hx.at[g, p], hx_s.at[g, d], hx_r.at[g, p], {"tp": p}).wait_recv()

        mid_rows = CLIP_RATIO * (jnp.max(hx[g, 0:n], axis=0) + EPSILON) / 127.0
        for e in range(experts):
            rows_m = 2 * sizes[g]
            coef[e, 0:rows_m, :] = jnp.broadcast_to(mid_rows[e:e + 1, 0:rows_m], (LANES, rows_m)).T

            def body(rows, info):
                mid = coef[e, rows, :]
                inv = 1.0 / mid
                for c, w in tiles:
                    scaled = h[e, rows, pl.ds(c, w)] * inv[:, 0:w]
                    hq[e, rows, pl.ds(c, w)] = jnp.clip(scaled, -127.0, 127.0).astype(BF16)
                coef[e, rows, :] = mid * spread(info[:, e:e + 1])

            row_blocks(g, body)

    def shard_of(k):
        return chunk(q - 1 - k % q, 1 - k // q)

    def rs_copy(g, k):
        return remote(
            ssend.at[k, rows_of(g), :], srecv.at[k, rows_of(g), :], rs_s.at[g, k], rs_r.at[g, k], sibling
        )

    def ry_copy(g, j):
        return remote(
            srecv.at[q - 1 - j, rows_of(g), :], yrecv.at[j, rows_of(g), :],
            ry_s.at[g, j], ry_r.at[g, j], partner,
        )

    def rz_copy(g, j):
        return remote(
            yrecv.at[j, rows_of(g), :], zrecv.at[z, rows_of(g), :],
            rz_s.at[g, j], rz_r.at[g, z], {"tp": chunk(j, 0)},
        )

    def combine(g, k):
        j = q - 1 - k % q
        rs_copy(g, k).wait_recv()
        mine = own[k % 2, 0:sizes[g], :]

        @pl.when(k < q)
        def _():
            srecv[k, rows_of(g), :] = (mine + srecv[k, rows_of(g), :].astype(F32)).astype(BF16)
            ry_copy(g, j).start()

        @pl.when(k >= q)
        def _():
            comb[j, rows_of(g), :] = mine + srecv[k, rows_of(g), :].astype(F32)

    def down(g, k):
        cols = chunk_rows(shard_of(k))
        rg = sizes[g]
        result = None
        for e in range(experts):
            part = jnp.dot(hq[e, 0:2 * rg, :], dbuf[e, :, cols], preferred_element_type=F32)
            part = part * coef[e, 0:2 * rg, 0:1] * ds_ref[:, cols][e:e + 1]
            result = part if result is None else result + part
        ssend[k, rows_of(g), :] = result[rg:].astype(BF16)
        rs_copy(g, k).start()
        own[k % 2, 0:rg, :] = result[0:rg]

        @pl.when(k > 0)
        def _():
            combine(g, k - 1)

    def finish(g, j):
        ry_copy(g, j).wait_recv()
        rows = rows_of(g)

        @pl.when(j > 0)
        def _():
            yrecv[j, rows, :] = (comb[j, rows, :] + yrecv[j, rows, :].astype(F32)).astype(BF16)
            rz_copy(g, j).start()

        @pl.when(j == 0)
        def _():
            comb[0, rows, :] += yrecv[0, rows, :].astype(F32)

    def final(g):
        rows = rows_of(g)

        @pl.loop(1, q)
        def _(j):
            s = z_of(j)
            part = zrecv.at[s, rows, :]
            remote(part, part, rz_s.at[g, j], rz_r.at[g, s], sibling).wait_recv()
            comb[0, rows, :] += zrecv[s, rows, :].astype(F32)

        out_ref[rows, :] = comb[0, rows, :].astype(BF16)

    per_step = -(-n // (q - 1))
    last = groups - 1
    for g in range(groups):

        @pl.loop(0, q)
        def _(t):
            @pl.when(t > 0)
            def _():
                if g < last:
                    across(g + 1, t)

            @pl.when(t == 0)
            def _():
                compute(g, 0, True)

            @pl.when(t > 0)
            def _():
                compute(g, 2 * t, False)

            if g + 2 <= last:

                @pl.when(t == 1)
                def _():
                    begin(g + 2)

            if g == 0:

                @pl.when(t + 1 < q)
                def _():
                    across(0, t + 1)

                beside(0, t)
            else:

                @pl.when(t == q - 1)
                def _():
                    beside(g, t)

            if g < last:

                @pl.when(t > 0)
                def _():
                    beside(g + 1, t - 1)

            compute(g, 2 * t + 1, False)

            if g > 0:

                @pl.when(t == 1)
                def _():
                    requantize(g - 1)

                @pl.when(t >= 1)
                def _():
                    @pl.loop(0, per_step)
                    def _(i):
                        k = (t - 1) * per_step + i

                        @pl.when(k < n)
                        def _():
                            down(g - 1, k)

            if g > 1:
                finish(g - 2, q - 1 - t)

        if g == 0:
            for e in range(experts):
                down_copy(e).wait()
        hidden(g)
        if g > 0:
            combine(g - 1, n - 1)

    requantize(last)

    @pl.loop(0, n)
    def _(k):
        down(last, k)
        if last > 0:

            @pl.when(k >= q)
            def _():
                finish(last - 1, n - 1 - k)

    combine(last, n - 1)

    @pl.loop(0, q)
    def _(i):
        finish(last, q - 1 - i)

    for g in range(groups):
        final(g)

    meta_copy.wait_send()

    @pl.loop(1, n)
    def _(d):
        pk_copy(d).wait_send()

    for g in range(groups):
        guard_own(lambda up: own_copy(g, up).wait_send())

        @pl.loop(1, n)
        def _(d):
            hx_copy(g, d).wait_send()

        @pl.loop(0, n)
        def _(k):
            sib_copy(g, k).wait_send()
            rs_copy(g, k).wait_send()

        @pl.loop(0, q)
        def _(j):
            y_copy(g, slab(j, 0)).wait_send()
            ry_copy(g, j).wait_send()

        @pl.loop(1, q)
        def _(j):
            guard_slabs(
                j, lambda p, step: guard_relay(g, p, step, lambda copy: copy.wait_send())
            )
            rz_copy(g, j).wait_send()


def per_device(
    n,
    tokens, smooth_in, expert_ids, gate_fixed, slots,
    w_gate, w_up, w_down, gate_scale, up_scale, smooth_mid, down_scale,
):
    q = n // 2
    experts, features, width = w_gate.shape
    block, depth = tokens.shape
    sizes = tuple(block * part // sum(SPLIT) for part in SPLIT)
    groups = len(sizes)
    rows_m = 2 * max(sizes)
    packed = width % LANES == 0
    halves = 1 if packed else 2
    cols = 2 * width if packed else width
    vmem = pl.BlockSpec(memory_space=pltpu.VMEM)
    hbm = pl.BlockSpec(memory_space=pl.ANY)
    dma = pltpu.SemaphoreType.DMA
    slab = (block, depth)
    return pl.pallas_call(
        functools.partial(kernel, n, 3 * block // 4, sizes),
        out_shape=jax.ShapeDtypeStruct((block, depth), BF16),
        in_specs=[vmem] * 5 + [hbm] * 3 + [vmem] * 4,
        out_specs=vmem,
        scratch_shapes=[
            pltpu.VMEM((n, 2, *slab), BF16),
            pltpu.VMEM((rows_m, depth), BF16),
            pltpu.VMEM((halves, experts, features, cols), BF16),
            pltpu.VMEM((experts, width, features), BF16),
            pltpu.VMEM((halves, experts, rows_m, cols), F32),
            pltpu.VMEM((experts, rows_m, width), F32),
            pltpu.VMEM((experts, rows_m, width), BF16),
            pltpu.VMEM((4, 8, block), F32),
            pltpu.VMEM((2, block, LANES), F32),
            pltpu.VMEM((experts, rows_m, LANES), F32),
            pltpu.VMEM((n + 8, 1, block + depth), F32),
            pltpu.VMEM((groups, n + 8, experts, rows_m), F32),
            pltpu.VMEM((rows_m, LANES), F32),
            pltpu.VMEM((2, max(sizes), depth), F32),
            pltpu.VMEM((n, *slab), BF16),
            pltpu.VMEM((n, *slab), BF16),
            pltpu.VMEM((q, *slab), F32),
            pltpu.VMEM((q, *slab), BF16),
            pltpu.VMEM((q, *slab), BF16),
            dma((n, 2)), dma((experts,)), dma((n,)), dma((n,)), dma((groups, n)), dma((groups, n)), dma, dma,
            dma((groups, 2)), dma((groups, q)), dma((groups, q)), dma((groups, n)), dma((groups, n)), dma((groups, n)),
            dma((groups, n)), dma((groups, n)), dma((groups, q)), dma((groups, q)), dma((groups, q)), dma((groups, q)),
        ],
        compiler_params=pltpu.CompilerParams(
            collective_id=0, has_side_effects=True, vmem_limit_bytes=67043328
        ),
    )(
        tokens, smooth_in[None, :], expert_ids.T, gate_fixed.T, slots.T,
        w_gate, w_up, w_down, gate_scale, up_scale, smooth_mid, down_scale,
    )


def solution(mesh):
    n = mesh.shape["tp"]
    in_specs = (
        P(("rep", "exp"), "tp"),
        P("tp"),
        P(("rep", "exp"), None),
        P(("rep", "exp"), None),
        P(("rep", "exp"), None),
        P("exp", None, "tp"),
        P("exp", None, "tp"),
        P("exp", "tp", None),
        P("exp", "tp"),
        P("exp", "tp"),
        P("exp", "tp"),
        P("exp", None),
    )
    out_specs = P(("rep", "exp"), "tp")
    return jax.shard_map(
        functools.partial(per_device, n), mesh=mesh, in_specs=in_specs, out_specs=out_specs, check_vma=False
    )
```

time: 107 us -> 97.8 us (0.914)
  Pallas kernels: 102 us -> 96 us
  other arithmetic: 2.26 us -> 0 us
    pallas_call x1, Pallas kernels: 102 us -> 96 us  [per_device(): pl.pallas_call(functools.partial(kernel, n, 3 * block // 4, sizes), out_s...]
where the time goes in v1:
time: 97.8 us; the launch traced here: 97.7 us
  Pallas kernels  96 us (98%)
  local copies, waits for them, and re-layouts  1.67 us (2%)
    pallas_call x1, Pallas kernels, per_device(): pl.pallas_call(functools.partial(kernel, n, 3 * block // 4, sizes), out_s...  96 us

profile of v1, /device:TPU:0, one launch (start us, length us, event | category | flops | bytes accessed | tf_op | source)
XLA Modules:
  0.0 97.7 jit_solution(16093654654846230615)
XLA Ops:
  0.0 96.0 %shard_map.118 = bf16[256,512]{1,0:T(8,128)(2,1)} custom-call(bf16[256,512]{1,0:T(8,128)(2,1)} %tok_ref.1, f32[1,512]{1,0:T(1,128)} %bitcast.4, s32[2,256]{1,0:T(2,128)} %bitcast.5, s32[2,256]{1,0:T(2,128)} %bitcast.6, s32[2,256]{1,0:T(2,128)} %bitcast.7, bf16[2,4096,896]{2,1,0:T(8,128)(2,1)} %wg_ref.1, bf16[2,4096,896]{2,1,0:T(8,128)(2,1)} %wu_ref.1, ...), custom_call_target="tpu_custom_call" | custom-call | tf_op jit(solution)/shard_map/pallas_call | solution.py:528
  96.0 1.7 %copy.14 = bf16[256,512]{1,0:T(8,128)(2,1)} copy(bf16[256,512]{1,0:T(8,128)(2,1)} %shard_map.118) | data formatting | bytes 524288

commit v2 on v1

--- a/solution.py
+++ b/solution.py
@@ -310,7 +310,7 @@
             row_blocks(g, body)
 
     def shard_of(k):
-        return chunk(q - 1 - k % q, 1 - k // q)
+        return slab(q - 1 - k % q, 1 - k // q)
 
     def rs_copy(g, k):
         return remote(
@@ -324,10 +324,18 @@
         )
 
     def rz_copy(g, j):
+        goal, step = line(j), side(j)
+        adjacent = (q + 1 - step * (goal - z)) // q
+        spot = goal + (1 - step) // 2 * adjacent * (q - goal)
         return remote(
-            yrecv.at[j, rows_of(g), :], zrecv.at[z, rows_of(g), :],
-            rz_s.at[g, j], rz_r.at[g, z], {"tp": chunk(j, 0)},
+            yrecv.at[j, rows_of(g), :], zrecv.at[spot, rows_of(g), :],
+            rz_s.at[g, j], rz_r.at[g, spot], {"tp": me + 2 * step},
         )
+
+    def landed(g, spot):
+        part = zrecv.at[spot, rows_of(g), :]
+        remote(part, part, rz_s.at[g, 0], rz_r.at[g, spot], sibling).wait_recv()
+        return zrecv[spot, rows_of(g), :].astype(F32)
 
     def combine(g, k):
         j = q - 1 - k % q
@@ -362,25 +370,29 @@
     def finish(g, j):
         ry_copy(g, j).wait_recv()
         rows = rows_of(g)
+        comb[j, rows, :] += yrecv[j, rows, :].astype(F32)
 
         @pl.when(j > 0)
         def _():
-            yrecv[j, rows, :] = (comb[j, rows, :] + yrecv[j, rows, :].astype(F32)).astype(BF16)
+            behind = z - side(j)
+
+            @pl.when((behind >= 0) & (behind < q))
+            def _():
+                comb[j, rows, :] += landed(g, line(j))
+
+            yrecv[j, rows, :] = comb[j, rows, :].astype(BF16)
             rz_copy(g, j).start()
-
-        @pl.when(j == 0)
-        def _():
-            comb[0, rows, :] += yrecv[0, rows, :].astype(F32)
 
     def final(g):
         rows = rows_of(g)
 
-        @pl.loop(1, q)
-        def _(j):
-            s = z_of(j)
-            part = zrecv.at[s, rows, :]
-            remote(part, part, rz_s.at[g, j], rz_r.at[g, s], sibling).wait_recv()
-            comb[0, rows, :] += zrecv[s, rows, :].astype(F32)
+        @pl.when(z > 0)
+        def _():
+            comb[0, rows, :] += landed(g, z)
+
+        @pl.when(z < q - 1)
+        def _():
+            comb[0, rows, :] += landed(g, q)
 
         out_ref[rows, :] = comb[0, rows, :].astype(BF16)
 
@@ -549,10 +561,10 @@
             pltpu.VMEM((n, *slab), BF16),
             pltpu.VMEM((q, *slab), F32),
             pltpu.VMEM((q, *slab), BF16),
-            pltpu.VMEM((q, *slab), BF16),
+            pltpu.VMEM((q + 1, *slab), BF16),
             dma((n, 2)), dma((experts,)), dma((n,)), dma((n,)), dma((groups, n)), dma((groups, n)), dma, dma,
             dma((groups, 2)), dma((groups, q)), dma((groups, q)), dma((groups, n)), dma((groups, n)), dma((groups, n)),
-            dma((groups, n)), dma((groups, n)), dma((groups, q)), dma((groups, q)), dma((groups, q)), dma((groups, q)),
+            dma((groups, n)), dma((groups, n)), dma((groups, q)), dma((groups, q)), dma((groups, q)), dma((groups, q + 1)),
         ],
         compiler_params=pltpu.CompilerParams(
             collective_id=0, has_side_effects=True, vmem_limit_bytes=67043328

time: 97.8 us -> 96 us (0.982)
  Pallas kernels: 96 us -> 94.2 us
    pallas_call x1, Pallas kernels: 96 us -> 94.2 us  [per_device(): pl.pallas_call(functools.partial(kernel, n, 3 * block // 4, sizes), out_s...]
where the time goes in v2:
time: 96 us; the launch traced here: 95.9 us
  Pallas kernels  94.2 us (98%)
  local copies, waits for them, and re-layouts  1.67 us (2%)
    pallas_call x1, Pallas kernels, per_device(): pl.pallas_call(functools.partial(kernel, n, 3 * block // 4, sizes), out_s...  94.2 us

profile of v2, /device:TPU:0, one launch (start us, length us, event | category | flops | bytes accessed | tf_op | source)
XLA Modules:
  0.0 95.9 jit_solution(6555198697665087993)
XLA Ops:
  0.0 94.2 %shard_map.118 = bf16[256,512]{1,0:T(8,128)(2,1)} custom-call(bf16[256,512]{1,0:T(8,128)(2,1)} %tok_ref.1, f32[1,512]{1,0:T(1,128)} %bitcast.4, s32[2,256]{1,0:T(2,128)} %bitcast.5, s32[2,256]{1,0:T(2,128)} %bitcast.6, s32[2,256]{1,0:T(2,128)} %bitcast.7, bf16[2,4096,896]{2,1,0:T(8,128)(2,1)} %wg_ref.1, bf16[2,4096,896]{2,1,0:T(8,128)(2,1)} %wu_ref.1, ...), custom_call_target="tpu_custom_call" | custom-call | tf_op jit(solution)/shard_map/pallas_call | solution.py:540
  94.2 1.7 %copy.14 = bf16[256,512]{1,0:T(8,128)(2,1)} copy(bf16[256,512]{1,0:T(8,128)(2,1)} %shard_map.118) | data formatting | bytes 524288
